TPU v7x, 32 devices: a whole 2x2x4 slice. The times are simulated.
32 devices in a mesh: expert: 4 (over y, core), tensor: 8 (over z, x).
Axes of the slice: x: 2, y: 2, z: 4, core: 2. Of those that a mesh axis runs over, the one named last changes fastest.
Arguments:
- tokens: bfloat16 [1024, 6144], P('expert'), may hold values from -6 to 6
- expert_ids: int32 [1024, 2], P('expert'), may hold values from 0 to 3, all different within a row; in each aligned block of 256 rows (0 to 255, 256 to 511, ...) at most 192 rows name the same one
- gate_weights: float32 [1024, 2], P('expert'), may hold values from 0.2 to 1
- w_gate: bfloat16 [4, 6144, 16384], P('expert', None, 'tensor'), may hold values from -0.078125 to 0.078125
- w_up: bfloat16 [4, 6144, 16384], P('expert', None, 'tensor'), may hold values from -0.078125 to 0.078125
- w_down: bfloat16 [4, 16384, 6144], P('expert', 'tensor'), may hold values from -0.0625 to 0.0625
Outputs:
- mixed: bfloat16 [1024, 6144], P(('expert', 'tensor'))
Inputs may be any that keep to these rules, and one draw needn't show every extreme that they name: `expert_ids`: each token names two different experts. Among the 256 tokens held at one index along `expert`, no expert is named by more than 192 tokens, and in some such blocks one expert is named by exactly 192.
All inputs are finite; a program needn't handle non-finite values.
Results may differ from a plain program's by a relative error of at most 0.005.
Values may be sent and summed in bfloat16 or wider, within the bound.
A program may use at most 192 MiB of HBM per device.

v0:
```python
import jax
import jax.numpy as jnp
from jax import lax
from jax.sharding import PartitionSpec as P

AXES = ("expert", "tensor")
CHUNKS = 2


def body(tokens, expert_ids, gate_weights, w_gate, w_up, w_down):
    tok_rows, width = tokens.shape
    experts = lax.axis_size("expert")
    parts = lax.axis_size("tensor")
    owned = tok_rows // parts
    piece = owned // CHUNKS
    me = lax.axis_index("expert")
    part = lax.axis_index("tensor")

    hot = expert_ids[:, :, None] == jnp.arange(experts, dtype=jnp.int32)[None, None, :]
    weight = jnp.sum(jnp.where(hot, gate_weights[:, :, None], 0.0), axis=1)
    weight = lax.all_gather(weight.T, "expert", axis=0)
    weight = lax.dynamic_index_in_dim(weight, me, axis=1, keepdims=False)
    weight = weight.reshape(experts * parts, CHUNKS, piece)

    rows = lax.dynamic_slice_in_dim(tokens, part * owned, owned, axis=0)
    gathered = [
        lax.all_gather(rows[c * piece:(c + 1) * piece], AXES, axis=0, tiled=True)
        for c in range(CHUNKS)
    ]
    results = []
    for c in range(CHUNKS):
        inputs = gathered[c]
        gate_proj = jnp.dot(inputs, w_gate[0], preferred_element_type=jnp.float32)
        up_proj = jnp.dot(inputs, w_up[0], preferred_element_type=jnp.float32)
        hidden = (jax.nn.silu(gate_proj) * up_proj).astype(jnp.bfloat16)
        out = jnp.dot(hidden, w_down[0], preferred_element_type=jnp.float32)
        out = (out * weight[:, c].reshape(-1)[:, None]).astype(jnp.bfloat16)
        results.append(lax.psum_scatter(out, AXES, scatter_dimension=0, tiled=True))
    return jnp.concatenate(results, axis=0).astype(jnp.bfloat16)


def solution(mesh):
    placed = (
        P("expert", None),
        P("expert", None),
        P("expert", None),
        P("expert", None, "tensor"),
        P("expert", None, "tensor"),
        P("expert", "tensor", None),
    )
    return jax.shard_map(
        body, mesh=mesh, in_specs=placed, out_specs=P(AXES, None), check_vma=False
    )
```

profile of v0, /device:TPU:0, one launch (start us, length us, event | category | flops | bytes accessed | tf_op | source)
XLA Modules:
  0.0 400.1 jit_solution(16893816836831131884)
XLA Ops:
  6.5 0.0 all-gather.5.cloned.1.call-start
  6.5 1.8 constant_dynamic-slice_fusion
  8.3 0.0 all-gather.5.cloned.1.call-update
  8.4 0.0 all-gather.7.cloned.1.call-start
  8.4 0.7 all-gather.7.cloned.1.call-update
  9.1 0.0 reduce-scatter.3.cloned.1.call-start
  9.2 0.7 select_reduce_fusion
  9.9 6.3 %all-gather.1 = f32[4,4,256]{2,1,0:T(4,128)S(1)} all-gather(f32[1,4,256]{2,1,0:T(4,128)S(1)} %bitcast.32), channel_id=2, replica_groups=mesh['expert'=4,'tensor'=8] {'expert'}, dimensions={0}, use_global_device_ids=true | all-gather | bytes 20480 | tf_op jit(solution)/shard_map/all_gather | solution.py:21
  16.2 0.1 reshape.8
  16.3 0.1 slice_reduce_fusion.1
  16.4 0.1 mul.39
  16.5 0.7 mul.44
  17.1 65.2 %all-gather.5.cloned.1.call-done = bf16[512,6144]{1,0:T(8,128)(2,1)} async-done(((bf16[16,6144]{1,0:T(8,128)(2,1)}), bf16[512,6144]{1,0:T(8,128)(2,1)}) %all-gather.5.cloned.1.call-update) | async-done | bytes 6291472 | tf_op jit(solution)/shard_map/all_gather | solution.py:27
  82.3 0.0 copy-start.2
  82.3 24.4 %fusion.10 = f32[512,2048]{1,0:T(8,128)} fusion(bf16[512,6144]{1,0:T(8,128)(2,1)} %all-gather.5.cloned.1.call-done, bf16[1,6144,2048]{2,1,0:T(8,128)(2,1)} %param.9), kind=kOutput, calls=%fused_computation.10 | convolution fusion | flops 12884901888 | bytes 35651584 | tf_op jit(solution)/shard_map/dot_general | solution.py:33
  106.8 0.0 copy-done.2
  106.8 19.1 %multiply_convert_fusion.3 = bf16[512,2048]{1,0:T(8,128)(2,1)S(1)} fusion(f32[512,2048]{1,0:T(8,128)} %fusion.10, bf16[512,6144]{1,0:T(8,128)(2,1)S(1)} %copy-done.2, bf16[1,6144,2048]{2,1,0:T(8,128)(2,1)} %param.10), kind=kOutput, calls=%fused_computation.15 | convolution fusion | flops 12891193344 | bytes 37748736 | tf_op jit(solution)/shard_map/dot_general | solution.py:34
  125.9 20.7 %multiply_convert_fusion.1 = bf16[512,6144]{1,0:T(8,128)(2,1)} fusion(bf16[512,2048]{1,0:T(8,128)(2,1)S(1)} %multiply_convert_fusion.3, bf16[1,2048,6144]{2,1,0:T(8,128)(2,1)} %param.11, f32[512]{0:T(512)S(1)} %mul.39), kind=kOutput, calls=%fused_computation.13 | convolution fusion | flops 12891193344 | bytes 33556480 | tf_op jit(solution)/shard_map/dot_general | solution.py:36
  146.6 0.0 reduce-scatter.3.cloned.1.call-update
  146.6 0.0 reduce-scatter.5.cloned.1.call-start
  146.7 6.5 %all-gather.7.cloned.1.call-done = bf16[512,6144]{1,0:T(8,128)(2,1)} async-done(((bf16[16,6144]{1,0:T(8,128)(2,1)}), bf16[512,6144]{1,0:T(8,128)(2,1)}) %all-gather.7.cloned.1.call-update) | async-done | bytes 6291472 | tf_op jit(solution)/shard_map/all_gather | solution.py:27
  153.2 0.0 copy-start.1
  153.2 24.4 %fusion.8 = f32[512,2048]{1,0:T(8,128)} fusion(bf16[512,6144]{1,0:T(8,128)(2,1)} %all-gather.7.cloned.1.call-done, bf16[1,6144,2048]{2,1,0:T(8,128)(2,1)} %param.9), kind=kOutput, calls=%fused_computation.8 | convolution fusion | flops 12884901888 | bytes 35651584 | tf_op jit(solution)/shard_map/dot_general | solution.py:33
  177.6 0.0 copy-done.1
  177.6 0.0 copy-start
  177.6 19.2 %multiply_convert_fusion.2 = bf16[512,2048]{1,0:T(8,128)(2,1)S(1)} fusion(f32[512,2048]{1,0:T(8,128)} %fusion.8, bf16[512,6144]{1,0:T(8,128)(2,1)S(1)} %copy-done.1, bf16[1,6144,2048]{2,1,0:T(8,128)(2,1)} %param.10), kind=kOutput, calls=%fused_computation.14 | convolution fusion | flops 12891193344 | bytes 37748736 | tf_op jit(solution)/shard_map/dot_general | solution.py:34
  196.8 0.0 copy-done
  196.8 19.9 %multiply_convert_fusion = bf16[512,6144]{1,0:T(8,128)(2,1)} fusion(bf16[512,2048]{1,0:T(8,128)(2,1)S(1)} %multiply_convert_fusion.2, bf16[1,2048,6144]{2,1,0:T(8,128)(2,1)} %param.11, f32[512]{0:T(512)S(1)} %copy-done), kind=kOutput, calls=%fused_computation.12 | convolution fusion | flops 12891193344 | bytes 33556480 | tf_op jit(solution)/shard_map/dot_general | solution.py:36
  216.7 0.0 reduce-scatter.5.cloned.1.call-update
  216.7 55.6 %reduce-scatter.3.cloned.1.call-done = bf16[16,6144]{1,0:T(8,128)(2,1)} async-done(((bf16[512,6144]{1,0:T(8,128)(2,1)}), bf16[16,6144]{1,0:T(8,128)(2,1)}) %reduce-scatter.3.cloned.1.call-update) | async-done | bytes 196624 | tf_op jit(solution)/shard_map/reduce_scatter | solution.py:38
  272.3 119.4 %reduce-scatter.5.cloned.1.call-done = bf16[16,6144]{1,0:T(8,128)(2,1)} async-done(((bf16[512,6144]{1,0:T(8,128)(2,1)}), bf16[16,6144]{1,0:T(8,128)(2,1)}) %reduce-scatter.5.cloned.1.call-update) | async-done | bytes 196624 | tf_op jit(solution)/shard_map/reduce_scatter | solution.py:38
  391.7 1.8 pad_maximum_fusion
  (1 shorter events, 0.0 us)
Async XLA Ops:
  6.5 75.8 %all-gather.5.cloned.1.call-start = ((), (), s32[]{:S(2)}) async-start(), calls=%async_computation.2 | async-start | bytes 6488064 | tf_op jit(solution)/shard_map/all_gather | solution.py:27
  8.4 144.8 %all-gather.7.cloned.1.call-start = ((), (), s32[]{:S(2)}) async-start(), calls=%async_computation.4 | async-start | bytes 6488064 | tf_op jit(solution)/shard_map/all_gather | solution.py:27
  9.1 263.2 %reduce-scatter.3.cloned.1.call-start = ((), (), s32[]{:S(2)}) async-start(), calls=%async_computation.3 | async-start | bytes 6488064 | tf_op jit(solution)/shard_map/reduce_scatter | solution.py:38
  82.3 24.4 %copy-start.2 = (bf16[512,6144]{1,0:T(8,128)(2,1)S(1)}, bf16[512,6144]{1,0:T(8,128)(2,1)}, u32[]{:S(2)}) copy-start(bf16[512,6144]{1,0:T(8,128)(2,1)} %all-gather.5.cloned.1.call-done) | copy-start | bytes 18874372
  146.6 245.1 %reduce-scatter.5.cloned.1.call-start = ((), (), s32[]{:S(2)}) async-start(), calls=%async_computation.5 | async-start | bytes 6488064 | tf_op jit(solution)/shard_map/reduce_scatter | solution.py:38
  153.2 24.4 %copy-start.1 = (bf16[512,6144]{1,0:T(8,128)(2,1)S(1)}, bf16[512,6144]{1,0:T(8,128)(2,1)}, u32[]{:S(2)}) copy-start(bf16[512,6144]{1,0:T(8,128)(2,1)} %all-gather.7.cloned.1.call-done) | copy-start | bytes 18874372
  177.6 19.2 %copy-start = (f32[512]{0:T(512)S(1)}, f32[512]{0:T(512)}, u32[]{:S(2)}) copy-start(f32[512]{0:T(512)} %mul.44) | copy-start | bytes 6148
Sparse Core Ops, SparseCore 0:
  10.3 71.9 all-gather.4
  85.3 67.7 all-gather.6
  158.8 113.4 reduce-scatter.2
  277.8 113.8 reduce-scatter.4
where the time goes:
time: 400 us
  waiting for transfers between devices  247 us (62%)
  matrix products  128 us (32%)
  between operations  13.2 us (3%)
  blocking collectives  6.27 us (2%)
    reduce_scatter x2, waiting for transfers between devices, body(): results.append(lax.psum_scatter(out, AXES, scatter_dimension=0, tiled=True))  175 us
    all_gather x2, waiting for transfers between devices, body(): lax.all_gather(rows[c * piece:(c + 1) * piece], AXES, axis=0, tiled=True)  71.7 us
    dot_general x2, matrix products, body(): gate_proj = jnp.dot(inputs, w_gate[0], preferred_element_type=jnp.float32)  48.8 us
    dot_general x2, matrix products, body(): out = jnp.dot(hidden, w_down[0], preferred_element_type=jnp.float32)  40.6 us
    dot_general x2, matrix products, body(): up_proj = jnp.dot(inputs, w_up[0], preferred_element_type=jnp.float32)  38.3 us
  transfers between devices with their start and end apart: 4, of which 4 were waited for; matrix products, arithmetic and copies ran while one was open for 32% of the time, Pallas kernels for 0%

commit v1 on v0

v1 whole, which is shorter than its diff:
```python
import functools

import jax
import jax.numpy as jnp
from jax import lax
from jax.experimental import pallas as pl
from jax.experimental.pallas import tpu as pltpu
from jax.sharding import PartitionSpec as P

MESH = pl.DeviceIdType.MESH
F32, BF16 = jnp.float32, jnp.bfloat16


def plan(events, ends):
    table = [[] for _ in range(len(ends) + 1)]
    for when, action in sorted(events, key=lambda item: item[0]):
        step = next((i for i, end in enumerate(ends) if end >= when), len(ends))
        table[step].append(action)
    return table


def moe_kernel(
    cfg,
    tok_hbm, wts, wg_hbm, wu_hbm, wd_hbm,
    out_ref,
    raw, xc, hid, wgu, wdn, keep, give, d2d_in, x_in, z_in, y_in, acc, rt, emat, wcol,
    s_tok, s_gu, s_dn, s_rt, s_pt, s_yp, s_zp, s_fy, s_fz, s_d2d, s_x, s_z, s_y,
):
    experts, parts, rows, cap, width, ff = cfg["dims"]
    ft, cw, pieces, slots = cfg["ft"], cfg["cw"], cfg["pieces"], cfg["slots"]
    pairs, nz, owned = experts // 2, parts // 2, rows // parts
    nch, nf, half = width // cw, ff // ft, rows // 2
    prow = half // pieces

    e = lax.axis_index("expert")
    t = lax.axis_index("tensor")
    yy, core = e // 2, e % 2
    z, x = t // 2, t % 2
    mate = e + 1 - 2 * core
    xmate = t + 1 - 2 * x
    z0 = z % 2
    zmate = t + 2 - 4 * z0

    def pair_dev(k):
        return ((yy + k + pairs) % pairs) * 2 + core

    def remote(src, dst, sems, index, dev):
        return pltpu.make_async_remote_copy(
            src_ref=src, dst_ref=dst, send_sem=sems.at[(0,) + index], recv_sem=sems.at[(1,) + index],
            device_id=dev, device_id_type=MESH)

    def route_copy(k):
        peer = (e + k) % experts
        return remote(wts.at[peer], rt.at[e], s_rt, (k - 1,), (peer, t))

    def mate_tokens():
        return remote(tok_hbm, raw.at[0, 1], s_pt, (), (mate, t))

    def piece_rows(which, p):
        return pl.ds(pl.multiple_of(which * half + p * prow, prow), prow)

    def y_piece(q, p):
        part = piece_rows(z0, p)
        return remote(tok_hbm.at[part], raw.at[q, 0, part], s_yp, (q - 1, p), (pair_dev(-q), t))

    def z_piece(q, p):
        part = piece_rows(z0, p)
        return remote(raw.at[q, 0, part], raw.at[q, 0, part], s_zp, (q - 1, p), (e, zmate))

    def fwd_y(q, p):
        part = piece_rows(z0, p)
        return remote(raw.at[q, 0, part], raw.at[q, 1, part], s_fy, (q - 1, p), (mate, t))

    def fwd_z(q, p):
        part = piece_rows(1 - z0, p)
        return remote(raw.at[q, 0, part], raw.at[q, 1, part], s_fz, (q - 1, p), (mate, t))

    def d2d(q, c):
        return remote(give.at[c], d2d_in.at[q, c], s_d2d, (q, c), (mate, t))

    def xsend(q, c):
        return remote(keep.at[q, c, :, 1 - x], x_in.at[q, c], s_x, (q, c), (e, xmate))

    def zsend(q, c, k):
        to = (z + k) % nz
        return remote(keep.at[q, c, to, x], z_in.at[q, c, k - 1], s_z, (q, c), (e, to * 2 + x))

    def zall(q, c):
        return remote(z_in.at[q, c], z_in.at[q, c], s_z, (q, c), (e, xmate))

    def ysend(q, c):
        return remote(keep.at[q, c, z, x], y_in.at[q - 1, c], s_y, (q - 1, c), (pair_dev(q), t))

    def gu_load(j, slot):
        cols = pl.ds(pl.multiple_of(j * ft, ft), ft)
        return [pltpu.make_async_copy(src.at[:, cols], wgu.at[slot, i], s_gu.at[slot, i])
                for i, src in enumerate((wg_hbm, wu_hbm))]

    def dn_load(c, slot):
        cols = pl.ds(pl.multiple_of(c * cw, cw), cw)
        return pltpu.make_async_copy(wd_hbm.at[:, cols], wdn.at[slot], s_dn.at[slot])

    def stage_mate(q, c):
        d2d(q, c).wait_recv()
        keep[q, c] = (keep[q, c].astype(F32) + d2d_in[q, c].astype(F32)).astype(BF16)
        xsend(q, c).start()

    def stage_x(q, c):
        xsend(q, c).wait_recv()
        total = keep[q, c, :, x].astype(F32) + x_in[q, c].astype(F32)
        keep[q, c, :, x] = total.astype(BF16)
        for k in range(1, nz):
            zsend(q, c, k).start()

    def stage_z(q, c):
        zall(q, c).wait_recv()
        total = keep[q, c, z, x].astype(F32)
        for k in range(1, nz):
            total += z_in[q, c, k - 1].astype(F32)
        if q == 0:
            acc[c] = total
        else:
            zall(q, c).wait_send()
            keep[q, c, z, x] = total.astype(BF16)
            ysend(q, c).start()

    def stage_y(c):
        total = acc[c]
        for q in range(1, pairs):
            ysend(q, c).wait_recv()
            total += y_in[q - 1, c].astype(F32)
        out_ref[:, pl.ds(pl.multiple_of(c * cw, cw), cw)] = total.astype(out_ref.dtype)

    own_tok = pltpu.make_async_copy(tok_hbm, raw.at[0, 0], s_tok)
    own_tok.start()
    for slot in range(2):
        for copy in gu_load(slot % nf, slot):
            copy.start()
    for slot in range(slots):
        dn_load(slot % nch, slot).start()

    barrier = pltpu.get_barrier_semaphore()
    peers = [((e + k) % experts, t) for k in range(1, experts)] + [(e, xmate)]
    peers += [(e, ((z + k) % nz) * 2 + x) for k in range(1, nz)]
    for peer in peers:
        pl.semaphore_signal(barrier, inc=1, device_id=peer, device_id_type=MESH)
    pl.semaphore_wait(barrier, len(peers))

    mate_tokens().start()
    for k in range(1, experts):
        route_copy(k).start()
    for p in range(pieces):
        for q in range(1, pairs):
            y_piece(q, p).start()
    rt[e] = wts[e]
    for k in range(1, experts):
        back = (e + experts - k) % experts
        remote(wts.at[back], rt.at[back], s_rt, (k - 1,), (back, t)).wait_recv()

    def compact(q, slot):
        block = ((yy + q) % pairs) * 2 + (core if slot == 0 else 1 - core)
        w = rt[block]
        mask = jnp.where(w > 0, 1.0, 0.0).astype(BF16)
        upto = lax.broadcasted_iota(jnp.int32, (rows, rows), 0)
        here = lax.broadcasted_iota(jnp.int32, (rows, rows), 1)
        before = jnp.where(upto <= here, 1.0, 0.0).astype(BF16)
        place = jnp.dot(mask, before, preferred_element_type=F32)
        place = jnp.where(w > 0, place - 1.0, -1.0)[:1]
        lane = lax.broadcasted_iota(jnp.int32, (cap, rows), 0).astype(F32)
        pick = jnp.broadcast_to(place, (cap, rows)) == lane
        wcol[slot] = jnp.broadcast_to(
            jnp.sum(jnp.where(pick, jnp.broadcast_to(w[:1], (cap, rows)), 0.0), axis=1, keepdims=True), (cap, 128))
        pick = jnp.where(pick, 1.0, 0.0).astype(BF16)
        after = jnp.where(here <= upto, 1.0, 0.0).astype(BF16)
        same = jnp.where(here == upto, 1.0, 0.0).astype(BF16)
        nt = (((1,), (1,)), ((), ()))
        place_col = lax.dot_general(after, mask, nt, preferred_element_type=F32)[:, :1]
        mask_col = lax.dot_general(same, mask, nt, preferred_element_type=F32)[:, :1]
        place_col = jnp.where(mask_col > 0.5, place_col - 1.0, -1.0)
        column = lax.broadcasted_iota(jnp.int32, (rows, cap), 1).astype(F32)
        emat[slot] = jnp.where(jnp.broadcast_to(place_col, (rows, cap)) == column, 1.0, 0.0).astype(BF16)

        if q == 0 and slot == 0:
            own_tok.wait()
        elif q == 0:
            mate_tokens().wait_recv()
        elif slot == 1:
            for p in range(pieces):
                fwd_y(q, p).wait_recv()
                fwd_z(q, p).wait_recv()

        @pl.loop(0, nch)
        def _(c):
            cols = pl.ds(pl.multiple_of(c * cw, cw), cw)
            got = jnp.dot(pick, raw[q, slot, :, cols], preferred_element_type=F32)
            xc[slot * cap:(slot + 1) * cap, cols] = got.astype(BF16)

    gu_t, per_x = cfg["gu_t"], cfg["per_x"]
    pass_t = nf * gu_t + nch
    gu_end = [(j + 1) * gu_t for j in range(nf)]
    dn_end = [nf * gu_t + j + 1 for j in range(nch)]

    def gather_events(q):
        events = []
        for p in range(pieces):
            arrive = cfg["y0"] + cfg["y_t"] * (p + 1)

            def one(p=p):
                y_piece(q, p).wait_recv()
                z_piece(q, p).start()
                fwd_y(q, p).start()

            def two(p=p):
                z_piece(q, p).wait_recv()
                fwd_z(q, p).start()

            events.append((arrive, one))
            events.append((arrive + cfg["y_t"] + cfg["hop"] + 0.5 * gu_t, two))
        return events

    def run(actions):
        for action in actions:
            action()

    for q in range(pairs):
        events = []
        if q == 0:
            for k in range(1, pairs):
                events += gather_events(k)
        else:
            start = -nch - cfg["lag"]
            for c in range(nch):
                at = start + cfg["hop"] + per_x * (c + 1)
                events.append((at, functools.partial(stage_x, q - 1, c)))
                events.append((max(at + cfg["z_t"], nf * gu_t + c + 0.5), functools.partial(stage_z, q - 1, c)))
        for c in range(nch):
            events.append((nf * gu_t + c + 2.5, functools.partial(stage_mate, q, c)))
        table = plan(events, gu_end + dn_end)

        for slot in range(2):
            compact(q, slot)

        @pl.loop(0, nf)
        def _(j):
            slot = j % 2
            for copy in gu_load(j, slot):
                copy.wait()
            gate = jnp.dot(xc[...], wgu[slot, 0], preferred_element_type=F32)
            up = jnp.dot(xc[...], wgu[slot, 1], preferred_element_type=F32)
            hid[:, pl.ds(pl.multiple_of(j * ft, ft), ft)] = (gate * (1.0 / (1.0 + jnp.exp(-gate))) * up).astype(BF16)

            @pl.when(j + 2 < nf)
            def _():
                for copy in gu_load(j + 2, slot):
                    copy.start()

            for step in range(nf):
                if table[step]:
                    pl.when(j == step)(functools.partial(run, table[step]))

        if q + 1 < pairs:
            for slot in range(2):
                for copy in gu_load(slot % nf, slot):
                    copy.start()

        @pl.loop(0, nch)
        def _(c):
            slot = c % slots
            dn_load(c, slot).wait()
            y = jnp.dot(hid[...], wdn[slot], preferred_element_type=F32)
            y0 = (y[:cap] * wcol[0, :, :1]).astype(BF16)
            y1 = (y[cap:] * wcol[1, :, :1]).astype(BF16)
            if q > 0:
                d2d(q - 1, c).wait_send()
            give[c] = jnp.dot(emat[1], y1, preferred_element_type=F32).astype(BF16).reshape(nz, 2, owned, cw)
            d2d(q, c).start()
            keep[q, c] = jnp.dot(emat[0], y0, preferred_element_type=F32).astype(BF16).reshape(nz, 2, owned, cw)

            ahead = c + slots
            if q + 1 < pairs:
                dn_load(ahead % nch, slot).start()
            else:
                @pl.when(ahead < nch)
                def _():
                    dn_load(ahead, slot).start()

            for step in range(nch):
                if table[nf + step]:
                    pl.when(c == step)(functools.partial(run, table[nf + step]))

        run(table[nf + nch])

    last = pairs - 1

    @pl.loop(0, nch + 4)
    def _(n):
        @pl.when(n < nch)
        def _():
            stage_x(last, n)

        @pl.when((n >= 2) & (n < nch + 2))
        def _():
            stage_z(last, n - 2)

        @pl.when(n >= 4)
        def _():
            stage_y(n - 4)

    mate_tokens().wait_send()
    for k in range(1, experts):
        route_copy(k).wait_send()
    for q in range(1, pairs):
        for p in range(pieces):
            for copy in (y_piece, z_piece, fwd_y, fwd_z):
                copy(q, p).wait_send()

    @pl.loop(0, nch)
    def _(c):
        d2d(last, c).wait_send()
        for q in range(pairs):
            xsend(q, c).wait_send()
            if q == 0:
                zall(q, c).wait_send()
            else:
                ysend(q, c).wait_send()


def body(tokens, expert_ids, gate_weights, w_gate, w_up, w_down):
    rows, width = tokens.shape
    experts = lax.axis_size("expert")
    parts = lax.axis_size("tensor")
    ff = w_gate.shape[2]
    cap = rows * 3 // 4
    pairs, nz, owned = experts // 2, parts // 2, rows // parts
    ft, cw, pieces, slots = 256, 512, 8, 3
    nch = width // cw
    others = pairs - 1

    hot = expert_ids[None, :, :] == jnp.arange(experts, dtype=jnp.int32)[:, None, None]
    weight = jnp.sum(jnp.where(hot, gate_weights[None], 0.0), axis=2)
    weight = jnp.broadcast_to(weight[:, None, :], (experts, 8, rows))

    cfg = dict(
        dims=(experts, parts, rows, cap, width, ff), ft=ft, cw=cw, pieces=pieces, slots=slots,
        gu_t=2.75, per_x=3.0, y0=-2.0, y_t=4.5, hop=2.0, lag=4.0, z_t=6.0,
    )
    dma = pltpu.SemaphoreType.DMA
    any_space = pl.BlockSpec(memory_space=pl.ANY)
    vmem = pl.BlockSpec(memory_space=pltpu.VMEM)
    return pl.pallas_call(
        functools.partial(moe_kernel, cfg),
        out_shape=jax.ShapeDtypeStruct((owned, width), BF16),
        in_specs=[any_space, vmem, any_space, any_space, any_space],
        out_specs=vmem,
        scratch_shapes=[
            pltpu.VMEM((pairs, 2, rows, width), BF16),
            pltpu.VMEM((2 * cap, width), BF16),
            pltpu.VMEM((2 * cap, ff), BF16),
            pltpu.VMEM((2, 2, width, ft), BF16),
            pltpu.VMEM((slots, ff, cw), BF16),
            pltpu.VMEM((pairs, nch, nz, 2, owned, cw), BF16),
            pltpu.VMEM((nch, nz, 2, owned, cw), BF16),
            pltpu.VMEM((pairs, nch, nz, 2, owned, cw), BF16),
            pltpu.VMEM((pairs, nch, nz, owned, cw), BF16),
            pltpu.VMEM((pairs, nch, nz - 1, owned, cw), BF16),
            pltpu.VMEM((others, nch, owned, cw), BF16),
            pltpu.VMEM((nch, owned, cw), F32),
            pltpu.VMEM((experts, 8, rows), F32),
            pltpu.VMEM((2, rows, cap), BF16),
            pltpu.VMEM((2, cap, 128), F32),
            dma,
            dma((2, 2)),
            dma((slots,)),
            dma((2, experts - 1)),
            dma((2,)),
            dma((2, others, pieces)),
            dma((2, others, pieces)),
            dma((2, others, pieces)),
            dma((2, others, pieces)),
            dma((2, pairs, nch)),
            dma((2, pairs, nch)),
            dma((2, pairs, nch)),
            dma((2, others, nch)),
        ],
        compiler_params=pltpu.CompilerParams(
            collective_id=0, has_side_effects=True, vmem_limit_bytes=67043328),
    )(tokens, weight, w_gate[0], w_up[0], w_down[0])


def solution(mesh):
    placed = (
        P("expert", None),
        P("expert", None),
        P("expert", None),
        P("expert", None, "tensor"),
        P("expert", None, "tensor"),
        P("expert", "tensor", None),
    )
    return jax.shard_map(
        body, mesh=mesh, in_specs=placed, out_specs=P(("expert", "tensor"), None), check_vma=False
    )
```

time: 400 us -> 157 us (0.39)
  waiting for transfers between devices: 247 us -> 0 us
  Pallas kernels: 0 us -> 153 us
  matrix products: 128 us -> 0 us
  between operations: 13.2 us -> 0.01 us
  blocking collectives: 6.27 us -> 0 us
    reduce_scatter x2 -> x0, waiting for transfers between devices: 175 us -> none  [body(): results.append(lax.psum_scatter(out, AXES, scatter_dimension=0, tiled=True))]
    pallas_call x0 -> x1, Pallas kernels: none -> 153 us  [body(): pl.pallas_call(functools.partial(moe_kernel, cfg), out_shape=jax.ShapeDty...]
    dot_general x6 -> x0, matrix products: 128 us -> none  [the longest x2 48.8 us: body(): gate_proj = jnp.dot(inputs, w_gate[0], preferred_element_type=jnp.float32)]
    all_gather x2 -> x0, waiting for transfers between devices: 71.7 us -> none  [body(): lax.all_gather(rows[c * piece:(c + 1) * piece], AXES, axis=0, tiled=True)]
    all_gather x1 -> x0, blocking collectives: 6.27 us -> none  [body(): weight = lax.all_gather(weight.T, 'expert', axis=0)]
  transfers between devices with their start and end apart: 4 -> 0, of which waited for: 4 -> 0; matrix products, arithmetic and copies ran while one was open for 32% -> 0% of each run, Pallas kernels for 0% -> 0%
where the time goes in v1:
time: 157 us; the launch traced here: 156 us
  Pallas kernels  153 us (97%)
  local copies, waits for them, and re-layouts  2.39 us (2%)
    pallas_call x1, Pallas kernels, body(): pl.pallas_call(functools.partial(moe_kernel, cfg), out_shape=jax.ShapeDty...  153 us

profile of v1, /device:TPU:0, one launch (start us, length us, event | category | flops | bytes accessed | tf_op | source)
XLA Modules:
  0.0 156.4 jit_solution(721496624841493238)
XLA Ops:
  0.0 0.7 select_reduce_fusion
  0.7 0.6 broadcast_in_dim.23.wts
  1.3 153.3 %shard_map.64 = bf16[32,6144]{1,0:T(8,128)(2,1)} custom-call(bf16[256,6144]{1,0:T(8,128)(2,1)} %tok_hbm.1, f32[4,8,256]{2,1,0:T(8,128)} %broadcast_in_dim.23.wts, bf16[6144,2048]{1,0:T(8,128)(2,1)} %bitcast.3, bf16[6144,2048]{1,0:T(8,128)(2,1)} %bitcast.4, bf16[2048,6144]{1,0:T(8,128)(2,1)} %bitcast.5), custom_call_target="tpu_custom_call" | custom-call | tf_op jit(solution)/shard_map/pallas_call | solution.py:350
  154.7 1.8 %copy.10 = bf16[32,6144]{1,0:T(8,128)(2,1)} copy(bf16[32,6144]{1,0:T(8,128)(2,1)} %shard_map.64) | data formatting | bytes 786432

commit v2 on v1

v2 whole, which is shorter than its diff:
```python
import functools

import jax
import jax.numpy as jnp
from jax import lax
from jax.experimental import pallas as pl
from jax.experimental.pallas import tpu as pltpu
from jax.sharding import PartitionSpec as P

MESH = pl.DeviceIdType.MESH
F32, BF16 = jnp.float32, jnp.bfloat16


def plan(events, ends):
    table = [[] for _ in range(len(ends) + 1)]
    for when, action in sorted(events, key=lambda item: item[0]):
        step = next((i for i, end in enumerate(ends) if end >= when), len(ends))
        table[step].append(action)
    return table


def moe_kernel(
    cfg,
    tok_hbm, wts, wg_hbm, wu_hbm, wd_hbm,
    out_ref,
    raw, xc, hid, wgu, wdn, ys, keep, give, d2d_in, x_in, za_in, z_in, y_in, acc, rt, emat, wcol,
    s_tok, s_gu, s_dn, s_rt, s_pt, s_yp, s_xp, s_zp, s_dg, s_fw, s_d2d, s_x, s_za, s_z, s_y,
):
    experts, parts, rows, cap, width, ff = cfg["dims"]
    ft, cw, pieces, slots = cfg["ft"], cfg["cw"], cfg["pieces"], cfg["slots"]
    pairs, nz, owned = experts // 2, parts // 2, rows // parts
    nch, nf, quarter = width // cw, ff // ft, rows // 4
    prow = quarter // pieces

    e = lax.axis_index("expert")
    t = lax.axis_index("tensor")
    yy, core = e // 2, e % 2
    z, x = t // 2, t % 2
    mate = e + 1 - 2 * core
    xmate = t + 1 - 2 * x
    z0 = z % 2
    zmate = t + 2 - 4 * z0
    z1, nz1 = z // 2, nz // 2

    def pair_dev(k):
        return ((yy + k + pairs) % pairs) * 2 + core

    def remote(src, dst, sems, index, dev):
        return pltpu.make_async_remote_copy(
            src_ref=src, dst_ref=dst, send_sem=sems.at[(0,) + index], recv_sem=sems.at[(1,) + index],
            device_id=dev, device_id_type=MESH)

    def route_copy(k):
        peer = (e + k) % experts
        return remote(wts.at[peer], rt.at[e], s_rt, (k - 1,), (peer, t))

    def mate_tokens():
        return remote(tok_hbm, raw.at[0, 1], s_pt, (), (mate, t))

    quarters = (2 * z0 + x, 2 * z0 + 1 - x, 2 * (1 - z0) + x, 2 * (1 - z0) + 1 - x)

    def piece_rows(kind, p):
        return pl.ds(pl.multiple_of(quarters[kind] * quarter + p * prow, prow), prow)

    def y_piece(q, p):
        part = piece_rows(0, p)
        return remote(tok_hbm.at[part], raw.at[q, 0, part], s_yp, (q - 1, p), (pair_dev(-q), t))

    def along(q, part, sems, p, dev):
        return remote(raw.at[q, 0, part], raw.at[q, 0, part], sems, (q - 1, p), dev)

    def x_piece(q, p):
        return along(q, piece_rows(0, p), s_xp, p, (e, xmate))

    def z_piece(q, p):
        return along(q, piece_rows(0, p), s_zp, p, (e, zmate))

    def diagonal(q, p):
        if p % 2 == 0:
            return along(q, piece_rows(2, p), s_dg, p, (e, xmate))
        return along(q, piece_rows(1, p), s_dg, p, (e, zmate))

    def forward(q, kind, p):
        part = piece_rows(kind, p)
        return remote(raw.at[q, 0, part], raw.at[q, 1, part], s_fw, (q - 1, kind * pieces + p), (mate, t))

    def d2d(q, c):
        return remote(give.at[c], d2d_in.at[q, c], s_d2d, (q, c), (mate, t))

    def xsend(q, c):
        return remote(keep.at[q, c, :, :, 1 - x], x_in.at[q, c], s_x, (q, c), (e, xmate))

    def zswap(q, c):
        return remote(keep.at[q, c, :, 1 - z0, x], za_in.at[q, c], s_za, (q, c), (e, zmate))

    def zsend(q, c, k):
        to = (z1 + k) % nz1
        return remote(keep.at[q, c, to, z0, x], z_in.at[q, c, k - 1], s_z, (q, c), (e, (to * 2 + z0) * 2 + x))

    def zall(q, c):
        return remote(z_in.at[q, c], z_in.at[q, c], s_z, (q, c), (e, xmate))

    def ysend(q, c):
        return remote(keep.at[q, c, z1, z0, x], y_in.at[q - 1, c], s_y, (q - 1, c), (pair_dev(q), t))

    def gu_load(j, slot):
        cols = pl.ds(pl.multiple_of(j * ft, ft), ft)
        return [pltpu.make_async_copy(src.at[:, cols], wgu.at[slot, i], s_gu.at[slot, i])
                for i, src in enumerate((wg_hbm, wu_hbm))]

    def dn_load(c, slot):
        cols = pl.ds(pl.multiple_of(c * cw, cw), cw)
        return pltpu.make_async_copy(wd_hbm.at[:, cols], wdn.at[slot], s_dn.at[slot])

    def stage_mate(q, c):
        d2d(q, c).wait_recv()
        keep[q, c] = (keep[q, c].astype(F32) + d2d_in[q, c].astype(F32)).astype(BF16)
        xsend(q, c).start()

    def stage_x(q, c):
        xsend(q, c).wait_recv()
        total = keep[q, c, :, :, x].astype(F32) + x_in[q, c].astype(F32)
        keep[q, c, :, :, x] = total.astype(BF16)
        zswap(q, c).start()

    def stage_swap(q, c):
        zswap(q, c).wait_recv()
        total = keep[q, c, :, z0, x].astype(F32) + za_in[q, c].astype(F32)
        keep[q, c, :, z0, x] = total.astype(BF16)
        for k in range(1, nz1):
            zsend(q, c, k).start()

    def stage_z(q, c):
        zall(q, c).wait_recv()
        total = keep[q, c, z1, z0, x].astype(F32)
        for k in range(1, nz1):
            total += z_in[q, c, k - 1].astype(F32)
        if q == 0:
            acc[c] = total
        else:
            zall(q, c).wait_send()
            keep[q, c, z1, z0, x] = total.astype(BF16)
            ysend(q, c).start()

    def stage_y(c):
        total = acc[c]
        for q in range(1, pairs):
            ysend(q, c).wait_recv()
            total += y_in[q - 1, c].astype(F32)
        out_ref[:, pl.ds(pl.multiple_of(c * cw, cw), cw)] = total.astype(out_ref.dtype)

    own_tok = pltpu.make_async_copy(tok_hbm, raw.at[0, 0], s_tok)
    own_tok.start()
    for copy in gu_load(0, 0):
        copy.start()
    rt[e] = wts[e]
    barrier = pltpu.get_barrier_semaphore()
    peers = [((e + k) % experts, t) for k in range(1, experts)] + [(e, xmate)]
    peers += [(e, ((z + k) % nz) * 2 + x) for k in range(1, nz)]
    for peer in peers:
        pl.semaphore_signal(barrier, inc=1, device_id=peer, device_id_type=MESH)

    def greet():
        pl.semaphore_wait(barrier, len(peers))
        for k in range(1, experts):
            route_copy(k).start()
        mate_tokens().start()
        for p in range(pieces):
            for q in range(1, pairs):
                y_piece(q, p).start()
        for slot in range(slots):
            dn_load(slot % nch, slot).start()

    def routes():
        for k in range(1, experts):
            back = (e + experts - k) % experts
            remote(wts.at[back], rt.at[back], s_rt, (k - 1,), (back, t)).wait_recv()

    def compact(q, slot):
        block = ((yy + q) % pairs) * 2 + (core if slot == 0 else 1 - core)
        w = rt[block]
        mask = jnp.where(w > 0, 1.0, 0.0).astype(BF16)
        upto = lax.broadcasted_iota(jnp.int32, (rows, rows), 0)
        here = lax.broadcasted_iota(jnp.int32, (rows, rows), 1)
        before = jnp.where(upto <= here, 1.0, 0.0).astype(BF16)
        place = jnp.dot(mask, before, preferred_element_type=F32)
        place = jnp.where(w > 0, place - 1.0, -1.0)[:1]
        lane = lax.broadcasted_iota(jnp.int32, (cap, rows), 0).astype(F32)
        pick = jnp.broadcast_to(place, (cap, rows)) == lane
        wcol[slot] = jnp.broadcast_to(
            jnp.sum(jnp.where(pick, jnp.broadcast_to(w[:1], (cap, rows)), 0.0), axis=1, keepdims=True), (cap, 128))
        pick = jnp.where(pick, 1.0, 0.0).astype(BF16)
        after = jnp.where(here <= upto, 1.0, 0.0).astype(BF16)
        same = jnp.where(here == upto, 1.0, 0.0).astype(BF16)
        nt = (((1,), (1,)), ((), ()))
        place_col = lax.dot_general(after, mask, nt, preferred_element_type=F32)[:, :1]
        mask_col = lax.dot_general(same, mask, nt, preferred_element_type=F32)[:, :1]
        place_col = jnp.where(mask_col > 0.5, place_col - 1.0, -1.0)
        column = lax.broadcasted_iota(jnp.int32, (rows, cap), 1).astype(F32)
        emat[slot] = jnp.where(jnp.broadcast_to(place_col, (rows, cap)) == column, 1.0, 0.0).astype(BF16)

        if q == 0 and slot == 0:
            own_tok.wait()
        elif q == 0:
            mate_tokens().wait_recv()
        elif slot == 1:
            for p in range(pieces):
                for kind in range(4):
                    forward(q, kind, p).wait_recv()

        wide = 4 * cw if nch % 4 == 0 else cw

        @pl.loop(0, width // wide)
        def _(c):
            cols = pl.ds(pl.multiple_of(c * wide, wide), wide)
            got = jnp.dot(pick, raw[q, slot, :, cols], preferred_element_type=F32)
            xc[slot * cap:(slot + 1) * cap, cols] = got.astype(BF16)

    gu_t, dn_t, hop, link, lags = cfg["gu_t"], cfg["dn_t"], cfg["hop"], cfg["link"], cfg["lags"]

    def settle(ends, when):
        return next((end for end in ends if end >= when), when)

    def gather_events(q, ends):
        events, queue, free, actions = [], [], {"x": 0.0, "z": 0.0}, {}
        piece = cfg["piece"]
        for p in range(pieces):
            def from_y(p=p):
                y_piece(q, p).wait_recv()
                x_piece(q, p).start()
                z_piece(q, p).start()
                forward(q, 0, p).start()

            def from_x(p=p):
                x_piece(q, p).wait_recv()
                if p % 2 == 1:
                    diagonal(q, p).start()
                forward(q, 1, p).start()

            def from_z(p=p):
                z_piece(q, p).wait_recv()
                if p % 2 == 0:
                    diagonal(q, p).start()
                forward(q, 2, p).start()

            def from_both(p=p):
                diagonal(q, p).wait_recv()
                forward(q, 3, p).start()

            arrive = cfg["late"] + piece * (p + 1)
            events.append((arrive, from_y))
            queue += [(settle(ends, arrive), p, "x", "first"), (settle(ends, arrive), p, "z", "first")]
            actions.update({("x", "first", p): from_x, ("z", "first", p): from_z,
                            ("x", "then", p): from_both, ("z", "then", p): from_both})
        while queue:
            queue.sort()
            issue, p, wire, kind = queue.pop(0)
            free[wire] = max(issue, free[wire]) + piece
            events.append((free[wire] + hop, actions[(wire, kind, p)]))
            if kind == "first" and (p % 2 == 1) == (wire == "x"):
                queue.append((settle(ends, free[wire] + hop), p, "z" if wire == "x" else "x", "then"))
        return events

    def run(actions):
        for action in actions:
            action()

    last = pairs - 1
    ahead_x = min(2, nch)

    for q in range(pairs):
        begin = cfg["gu0"] if q == 0 else cfg["gu1"]
        skip = 2 if q == 0 else 0
        ends = [begin + max(0, j + 1 - skip) * gu_t for j in range(nf)]
        dn_at = ends[-1]
        ends += [dn_at + (j + 1) * dn_t for j in range(nch + 1)]
        events = []
        if q == 0:
            for k in range(1, pairs):
                events += gather_events(k, ends)
        else:
            for c in range(nch):
                at = lags[0] * dn_t + hop + link * (c + 1) + cfg["slack"]
                events.append((at, functools.partial(stage_x, q - 1, c)))
                at = settle(ends, at) + hop + 0.7 * link
                events.append((at, functools.partial(stage_swap, q - 1, c)))
                at = max(settle(ends, at) + hop + link, dn_at + (c - 1.5) * dn_t)
                events.append((at, functools.partial(stage_z, q - 1, c)))
        for c in range(nch):
            events.append((dn_at + (c + lags[min(q, 1)] - 0.5) * dn_t, functools.partial(stage_mate, q, c)))
        if q == last:
            for c in range(ahead_x):
                at = dn_at + lags[1] * dn_t + hop + link * (c + 1) + 1.5
                events.append((at, functools.partial(stage_x, q, c)))
        table = plan(events, ends)

        def gate_up(j, lo, hi):
            slot = j % 2
            gate = jnp.dot(xc[lo:hi], wgu[slot, 0], preferred_element_type=F32)
            up = jnp.dot(xc[lo:hi], wgu[slot, 1], preferred_element_type=F32)
            hidden = (gate * (1.0 / (1.0 + jnp.exp(-gate))) * up).astype(BF16)
            hid[lo:hi, pl.ds(pl.multiple_of(j * ft, ft), ft)] = hidden

        def gu_wait(j):
            for copy in gu_load(j, j % 2):
                copy.wait()

        def gu_refill(j):
            @pl.when(j + 2 < nf)
            def _():
                for copy in gu_load(j + 2, j % 2):
                    copy.start()

        if q == 0:
            compact(0, 0)
            for copy in gu_load(1, 1):
                copy.start()
            greet()

            @pl.loop(0, 2)
            def _(j):
                gu_wait(j)
                gate_up(j, 0, cap)

            routes()
            compact(0, 1)

            @pl.loop(0, 2)
            def _(j):
                gate_up(j, cap, 2 * cap)
                gu_refill(j)

            run(table[0])
            run(table[1])
        else:
            for slot in range(2):
                compact(q, slot)

        @pl.loop(skip, nf)
        def _(j):
            gu_wait(j)
            gate_up(j, 0, 2 * cap)
            gu_refill(j)
            for step in range(skip, nf):
                if table[step]:
                    pl.when(j == step)(functools.partial(run, table[step]))

        def expand():
            return [jnp.dot(emat[i], ys[i], preferred_element_type=F32).astype(BF16).reshape(nz1, 2, 2, owned, cw)
                    for i in range(2)]

        def put(c, values):
            keep[q, c], give[c] = values
            d2d(q, c).start()

        def project(slot):
            y = jnp.dot(hid[...], wdn[slot], preferred_element_type=F32)
            ys[0] = (y[:cap] * wcol[0, :, :1]).astype(BF16)
            ys[1] = (y[cap:] * wcol[1, :, :1]).astype(BF16)

        def refill(c, slot):
            ahead = c + slots
            if q + 1 < pairs:
                dn_load(ahead % nch, slot).start()
            else:
                @pl.when(ahead < nch)
                def _():
                    dn_load(ahead, slot).start()

        dn_load(0, 0).wait()
        project(0)
        refill(0, 0)
        run(table[nf])

        @pl.loop(1, nch)
        def _(c):
            slot = c % slots
            dn_load(c, slot).wait()
            if q > 0:
                d2d(q - 1, c - 1).wait_send()
            values = expand()
            keep[q, c - 1], give[c - 1] = values
            project(slot)
            d2d(q, c - 1).start()
            refill(c, slot)
            if q + 1 < pairs:
                for i in range(2):
                    for k, copy in enumerate(gu_load(i, i)):
                        pl.when(c == min(nch - 1, 1 + 2 * (2 * i + k)))(lambda copy=copy: copy.start())

            for step in range(1, nch):
                if table[nf + step]:
                    pl.when(c == step)(functools.partial(run, table[nf + step]))

        if q > 0:
            d2d(q - 1, nch - 1).wait_send()
        put(nch - 1, expand())
        run(table[nf + nch])
        run(table[nf + nch + 1])

    def sent(q, c):
        if q == last:
            d2d(q, c).wait_send()
        xsend(q, c).wait_send()
        zswap(q, c).wait_send()
        if q == 0:
            zall(q, c).wait_send()
        else:
            ysend(q, c).wait_send()

    def sent_tokens():
        mate_tokens().wait_send()
        for k in range(1, experts):
            route_copy(k).wait_send()
        for q in range(1, pairs):
            for p in range(pieces):
                for copy in (y_piece, x_piece, z_piece, diagonal):
                    copy(q, p).wait_send()
                for kind in range(4):
                    forward(q, kind, p).wait_send()

    @pl.loop(ahead_x, nch)
    def _(n):
        stage_x(last, n)

        @pl.when(n >= 2)
        def _():
            stage_swap(last, n - 2)

        @pl.when(n >= 5)
        def _():
            stage_z(last, n - 5)

        @pl.when(n >= 7)
        def _():
            stage_y(n - 7)

        for q in range(last):
            sent(q, n)
        pl.when(n == max(ahead_x, nch // 2))(sent_tokens)

    @pl.loop(max(0, nch - 2), nch)
    def _(n):
        stage_swap(last, n)

    @pl.loop(max(0, nch - 5), nch)
    def _(n):
        stage_z(last, n)

    @pl.loop(max(0, nch - 7), nch)
    def _(n):
        stage_y(n)

    for c in range(ahead_x):
        for q in range(last):
            sent(q, c)

    @pl.loop(0, nch)
    def _(c):
        sent(last, c)


def body(tokens, expert_ids, gate_weights, w_gate, w_up, w_down):
    rows, width = tokens.shape
    experts = lax.axis_size("expert")
    parts = lax.axis_size("tensor")
    ff = w_gate.shape[2]
    cap = rows * 3 // 4
    pairs, nz, owned = experts // 2, parts // 2, rows // parts
    ft, cw, pieces, slots = 256, 512, 4, 3
    nch = width // cw
    others = pairs - 1

    hot = expert_ids[None, :, :] == jnp.arange(experts, dtype=jnp.int32)[:, None, None]
    weight = jnp.sum(jnp.where(hot, gate_weights[None], 0.0), axis=2)
    weight = jnp.broadcast_to(weight[:, None, :], (experts, 8, rows))

    cfg = dict(
        dims=(experts, parts, rows, cap, width, ff), ft=ft, cw=cw, pieces=pieces, slots=slots,
        gu_t=2.7, dn_t=1.2, hop=1.9, link=2.85, lags=(8.0, 3.0), piece=4.3, gu0=9.8, gu1=20.0, late=3.0, slack=2.5,
    )
    dma = pltpu.SemaphoreType.DMA
    any_space = pl.BlockSpec(memory_space=pl.ANY)
    vmem = pl.BlockSpec(memory_space=pltpu.VMEM)
    return pl.pallas_call(
        functools.partial(moe_kernel, cfg),
        out_shape=jax.ShapeDtypeStruct((owned, width), BF16),
        in_specs=[any_space, vmem, any_space, any_space, any_space],
        out_specs=vmem,
        scratch_shapes=[
            pltpu.VMEM((pairs, 2, rows, width), BF16),
            pltpu.VMEM((2 * cap, width), BF16),
            pltpu.VMEM((2 * cap, ff), BF16),
            pltpu.VMEM((2, 2, width, ft), BF16),
            pltpu.VMEM((slots, ff, cw), BF16),
            pltpu.VMEM((2, cap, cw), BF16),
            pltpu.VMEM((pairs, nch, nz // 2, 2, 2, owned, cw), BF16),
            pltpu.VMEM((nch, nz // 2, 2, 2, owned, cw), BF16),
            pltpu.VMEM((pairs, nch, nz // 2, 2, 2, owned, cw), BF16),
            pltpu.VMEM((pairs, nch, nz // 2, 2, owned, cw), BF16),
            pltpu.VMEM((pairs, nch, nz // 2, owned, cw), BF16),
            pltpu.VMEM((pairs, nch, nz // 2 - 1, owned, cw), BF16),
            pltpu.VMEM((others, nch, owned, cw), BF16),
            pltpu.VMEM((nch, owned, cw), F32),
            pltpu.VMEM((experts, 8, rows), F32),
            pltpu.VMEM((2, rows, cap), BF16),
            pltpu.VMEM((2, cap, 128), F32),
            dma,
            dma((2, 2)),
            dma((slots,)),
            dma((2, experts - 1)),
            dma((2,)),
            dma((2, others, pieces)),
            dma((2, others, pieces)),
            dma((2, others, pieces)),
            dma((2, others, pieces)),
            dma((2, others, 4 * pieces)),
            dma((2, pairs, nch)),
            dma((2, pairs, nch)),
            dma((2, pairs, nch)),
            dma((2, pairs, nch)),
            dma((2, others, nch)),
        ],
        compiler_params=pltpu.CompilerParams(
            collective_id=0, has_side_effects=True, vmem_limit_bytes=67043328),
    )(tokens, weight, w_gate[0], w_up[0], w_down[0])


def solution(mesh):
    placed = (
        P("expert", None),
        P("expert", None),
        P("expert", None),
        P("expert", None, "tensor"),
        P("expert", None, "tensor"),
        P("expert", "tensor", None),
    )
    return jax.shard_map(
        body, mesh=mesh, in_specs=placed, out_specs=P(("expert", "tensor"), None), check_vma=False
    )
```

time: 157 us -> 139 us (0.89)
  Pallas kernels: 153 us -> 136 us
    pallas_call x1, Pallas kernels: 153 us -> 136 us  [body(): pl.pallas_call(functools.partial(moe_kernel, cfg), out_shape=jax.ShapeDty...]
where the time goes in v2:
time: 139 us
  Pallas kernels  136 us (98%)
  local copies, waits for them, and re-layouts  2.39 us (2%)
    pallas_call x1, Pallas kernels, body(): pl.pallas_call(functools.partial(moe_kernel, cfg), out_shape=jax.ShapeDty...  136 us

profile of v2, /device:TPU:0, one launch (start us, length us, event | category | flops | bytes accessed | tf_op | source)
XLA Modules:
  0.0 138.8 jit_solution(18145215177176720219)
XLA Ops:
  0.0 0.7 select_reduce_fusion
  0.7 0.6 broadcast_in_dim.23.wts
  1.3 135.7 %shard_map.64 = bf16[32,6144]{1,0:T(8,128)(2,1)} custom-call(bf16[256,6144]{1,0:T(8,128)(2,1)} %tok_hbm.1, f32[4,8,256]{2,1,0:T(8,128)} %broadcast_in_dim.23.wts, bf16[6144,2048]{1,0:T(8,128)(2,1)} %bitcast.3, bf16[6144,2048]{1,0:T(8,128)(2,1)} %bitcast.4, bf16[2048,6144]{1,0:T(8,128)(2,1)} %bitcast.5), custom_call_target="tpu_custom_call" | custom-call | tf_op jit(solution)/shard_map/pallas_call | solution.py:485
  137.1 1.8 %copy.10 = bf16[32,6144]{1,0:T(8,128)(2,1)} copy(bf16[32,6144]{1,0:T(8,128)(2,1)} %shard_map.64) | data formatting | bytes 786432
